TPU v7x, 32 devices: a whole 2x2x4 slice. The times are simulated.
32 devices in a mesh: terms: 2 (over x), rows: 4 (over y, core), cols: 4 (over z).
Axes of the slice: x: 2, y: 2, z: 4, core: 2. Of those that a mesh axis runs over, the one named last changes fastest.
Arguments:
- wavefunction: bfloat16 [2, 1024, 1024], P(None, 'rows', 'cols'), may hold values from -6 to 6
- energy: float32 [2], replicated, may hold values from 1 to 4
- block_rows: int32 [2], replicated, may hold values from 512 to 1024
- block_cols: int32 [2], replicated, may hold values from 512 to 1024
- left_ops: bfloat16 [8, 1024, 1024], P('terms', 'rows'), may hold values from -0.1875 to 0.1875
- right_ops: bfloat16 [8, 1024, 1024], P('terms', 'cols'), may hold values from -0.1875 to 0.1875
- source: int32 [8], P('terms'), may hold values from 0 to 1
- target: int32 [8], P('terms'), may hold values from 0 to 1
Outputs:
- sigma: bfloat16 [2, 1024, 1024], P(None, 'rows', 'cols')
- residual: bfloat16 [2, 1024, 1024], P(None, 'rows', 'cols')
Inputs may be any that keep to these rules, and one draw needn't show every extreme that they name: source[t] is the sector whose block term t reads. target[t] is the sector to which term t adds. `block_rows`: entries of a sector block beyond its live left or right states are ignored.
All inputs are finite; a program needn't handle non-finite values.
Results may differ from a plain program's by a relative error of at most 0.0044.
The roundings to bfloat16 on the way count: a program that leaves them out, or rounds other values in their place, can miss the bound.
Values may be sent and summed in bfloat16 or wider, within the bound.
No kernel may reach another device: no remote copies, remote signals or barrier semaphores. Data moves between devices by JAX's collectives and lax.ppermute only.
A program may use at most 64 MiB of HBM per device.

v0:
```python
import jax
import jax.numpy as jnp
from jax import lax
from jax.sharding import PartitionSpec as P

EPSILON = 1e-06


def per_device(wavefunction, energy, block_rows, block_cols, left_ops, right_ops, source, target):
    sectors, tile_rows, tile_cols = wavefunction.shape
    term_count = left_ops.shape[0]
    row_ids = lax.axis_index("rows") * tile_rows + lax.iota(jnp.int32, tile_rows)
    col_ids = lax.axis_index("cols") * tile_cols + lax.iota(jnp.int32, tile_cols)
    inside = (row_ids[None, :, None] < block_rows[:, None, None]) & (
        col_ids[None, None, :] < block_cols[:, None, None]
    )
    live_psi = jnp.where(inside, wavefunction, jnp.zeros_like(wavefunction))
    sector_ids = lax.iota(jnp.int32, sectors)
    partial_value = jnp.zeros((sectors, tile_rows, tile_cols), jnp.float32)
    panels = lax.all_gather(live_psi, "rows", axis=1, tiled=True)
    product_list = []
    for term_index in range(term_count):
        col_panel = lax.dynamic_index_in_dim(panels, source[term_index], 0, keepdims=False)
        product_list.append(
            jnp.dot(left_ops[term_index], col_panel, preferred_element_type=jnp.float32).astype(
                jnp.bfloat16
            )
        )
    products = jnp.stack(product_list)
    additions = jnp.einsum(
        "txl,tml->txm",
        lax.all_gather(products, "cols", axis=2, tiled=True),
        right_ops,
        preferred_element_type=jnp.float32,
    )
    for term_index in range(term_count):
        hit = (sector_ids == target[term_index])[:, None, None]
        partial_value = partial_value + jnp.where(hit, additions[term_index][None], 0.0)
    live_f = live_psi.astype(jnp.float32)
    summed = lax.psum(partial_value, "terms")
    full_sigma = jnp.where(inside, summed + energy[:, None, None] * live_f, 0.0)
    numerator, denominator = lax.psum(
        (jnp.sum(live_f * full_sigma), jnp.sum(live_f * live_f)), ("rows", "cols")
    )
    rayleigh = numerator / (denominator + EPSILON)
    residual = full_sigma - rayleigh * live_f
    return (full_sigma.astype(jnp.bfloat16), residual.astype(jnp.bfloat16))


def solution(mesh):
    in_specs = (
        P(None, "rows", "cols"),
        P(),
        P(),
        P(),
        P("terms", "rows", None),
        P("terms", "cols", None),
        P("terms"),
        P("terms"),
    )
    out_specs = (P(None, "rows", "cols"), P(None, "rows", "cols"))
    return jax.shard_map(
        per_device, mesh=mesh, in_specs=in_specs, out_specs=out_specs, check_vma=False
    )
```

profile of v0, /device:TPU:0, one launch (start us, length us, event | category | flops | bytes accessed | tf_op | source)
XLA Modules:
  0.0 158.2 jit_solution(4470335550946866538)
XLA Ops:
  7.2 0.0 copy-start
  7.2 0.0 all-gather.3.cloned.1.call-start
  7.3 0.9 broadcast_compare_fusion
  8.1 1.8 %and_select_fusion.1 = bf16[2,256,256]{2,1,0:T(8,128)(2,1)} fusion(bf16[2,256,256]{2,1,0:T(8,128)(2,1)} %param.8, pred[2,256]{1,0:T(4,128)(4,1)S(1)} %get-tuple-element.20, pred[2,256]{1,0:T(4,128)(4,1)S(1)} %get-tuple-element.21), kind=kLoop, calls=%fused_computation.13 | loop fusion | flops 262144 | bytes 525312 | tf_op jit(solution)/shard_map/jit(_where)/select_n | solution.py:17
  9.9 0.0 all-gather.3.cloned.1.call-update
  10.0 0.0 all-gather.5.cloned.1.call-start
  10.0 1.5 fusion.31
  19.3 10.4 %all-gather.3.cloned.1.call-done = bf16[2,1024,256]{2,1,0:T(8,128)(2,1)} async-done(((bf16[2,256,256]{2,1,0:T(8,128)(2,1)}), bf16[2,1024,256]{2,1,0:T(8,128)(2,1)}) %all-gather.3.cloned.1.call-update) | async-done | bytes 1048592 | tf_op jit(solution)/shard_map/all_gather | solution.py:20
  29.6 0.0 copy-start.4
  29.6 0.0 copy-start.5
  29.6 1.7 %fusion = bf16[1,256,256]{1,2,0:T(8,128)(2,1)S(1)} fusion(bf16[4,256,1024]{2,1,0:T(8,128)(2,1)} %param.12, bf16[2,1024,256]{2,1,0:T(8,128)(2,1)} %all-gather.3.cloned.1.call-done, s32[]{:T(128)S(6)} %select_n.35), kind=kOutput, calls=%fused_computation.4 | convolution fusion | flops 134283264 | bytes 1179652 | tf_op jit(solution)/shard_map/dot_general | solution.py:25
  31.3 1.6 fusion.1
  32.9 0.0 copy-done.4
  32.9 0.0 copy-start.2
  32.9 1.4 fusion.2
  34.3 0.0 copy-done.5
  34.3 0.4 fusion.3
  34.7 0.9 pad_maximum_fusion
  35.6 0.0 all-gather.5.cloned.1.call-update
  35.6 0.0 all-reduce.3.cloned.1.call-start
  35.6 0.0 copy-done.2
  35.7 0.6 fusion.30
  36.2 1.1 iota_compare_fusion
  37.4 1.3 iota_compare_fusion.2
  38.7 42.7 %all-gather.5.cloned.1.call-done = bf16[4,256,1024]{1,2,0:T(8,128)(2,1)} async-done(((bf16[4,256,256]{1,2,0:T(8,128)(2,1)}), bf16[4,256,1024]{1,2,0:T(8,128)(2,1)}) %all-gather.5.cloned.1.call-update) | async-done | bytes 2097168 | tf_op jit(solution)/shard_map/all_gather | solution.py:32
  81.4 0.0 copy-done
  81.4 2.4 %fusion.32 = f32[4,256,256]{2,1,0:T(8,128)S(1)} fusion(bf16[4,256,1024]{1,2,0:T(8,128)(2,1)} %all-gather.5.cloned.1.call-done, bf16[4,256,1024]{2,1,0:T(8,128)(2,1)S(1)} %copy-done), kind=kOutput, calls=%fused_computation.56 | convolution fusion | flops 536870912 | bytes 5242880 | tf_op jit(solution)/shard_map/txl,tml->txm/dot_general | solution.py:30
  83.9 0.0 copy-start.1
  83.9 0.0 copy-start.3
  83.9 0.1 slice_bitcast_fusion.3
  84.0 1.0 select_add_fusion
  85.0 0.0 all-reduce.3.cloned.1.call-update
  85.0 27.6 %all-reduce.3.cloned.1.call-done = f32[2,256,256]{2,1,0:T(8,128)} async-done(((f32[2,256,256]{2,1,0:T(8,128)}), f32[2,256,256]{2,1,0:T(8,128)}) %all-reduce.3.cloned.1.call-update) | async-done | bytes 524304 | tf_op jit(solution)/shard_map/psum | solution.py:40
  112.6 0.0 copy-done.1
  112.6 0.0 copy-done.3
  112.6 2.0 %fusion.6 = (f32[]{:T(128)}, f32[]{:T(128)}) fusion(f32[2,256,256]{2,1,0:T(8,128)} %all-reduce.3.cloned.1.call-done, f32[2]{0:T(128)S(1)} %copy-done.3, pred[2,256]{1,0:T(4,128)(4,1)S(1)} %get-tuple-element.20, pred[2,256]{1,0:T(4,128)(4,1)S(1)} %get-tuple-element.21, bf16[2,256,256]{2,1,0:T(8,128)(2,1)S(1)} %copy-done.1), kind=kLoop, calls=%fused_computation.16 | loop fusion | flops 1310718 | bytes 787472 | tf_op jit(solution)/shard_map/reduce_sum | solution.py:43
  114.6 33.8 %all-reduce = (f32[]{:T(128)}, f32[]{:T(128)}) all-reduce(f32[]{:T(128)} %get-tuple-element.3, f32[]{:T(128)} %get-tuple-element.2), channel_id=1, replica_groups=mesh['terms'=2,'rows'=4,'cols'=4] {'rows','cols'}, use_global_device_ids=true, to_apply=%region_2.3 | all-reduce | flops 2 | bytes 16 | tf_op jit(solution)/shard_map/psum | solution.py:42
  149.6 2.1 %fusion.8 = (bf16[2,256,256]{2,1,0:T(8,128)(2,1)}, bf16[2,256,256]{2,1,0:T(8,128)(2,1)}) fusion(f32[]{:T(128)S(6)} %div.3, f32[2,256,256]{2,1,0:T(8,128)} %all-reduce.3.cloned.1.call-done, f32[2]{0:T(128)S(1)} %copy-done.3, pred[2,256]{1,0:T(4,128)(4,1)S(1)} %get-tuple-element.20, pred[2,256]{1,0:T(4,128)(4,1)S(1)} %get-tuple-element.21, ...), kind=kLoop, calls=%fused_computation.18 | loop fusion | flops 1310720 | bytes 1311756 | tf_op jit(solution)/shard_map/convert_element_type | solution.py:47
  (2 shorter events, 0.0 us)
Async XLA Ops:
  7.2 74.2 %copy-start = (bf16[4,256,1024]{2,1,0:T(8,128)(2,1)S(1)}, bf16[4,256,1024]{2,1,0:T(8,128)(2,1)}, u32[]{:S(2)}) copy-start(bf16[4,256,1024]{2,1,0:T(8,128)(2,1)} %param.13) | copy-start | bytes 6291460
  7.2 22.4 %all-gather.3.cloned.1.call-start = ((), (), s32[]{:S(2)}) async-start(), calls=%async_computation | async-start | bytes 1310720 | tf_op jit(solution)/shard_map/all_gather | solution.py:20
  10.0 71.4 %all-gather.5.cloned.1.call-start = ((), (), s32[]{:S(2)}) async-start(), calls=%async_computation.1 | async-start | bytes 2621440 | tf_op jit(solution)/shard_map/all_gather | solution.py:32
  29.6 3.3 %copy-start.4 = (bf16[4,256,1024]{2,1,0:T(8,128)(2,1)S(1)}, bf16[4,256,1024]{2,1,0:T(8,128)(2,1)}, u32[]{:S(2)}) copy-start(bf16[4,256,1024]{2,1,0:T(8,128)(2,1)} %param.12) | copy-start | bytes 6291460
  29.6 4.7 %copy-start.5 = (bf16[2,1024,256]{2,1,0:T(8,128)(2,1)S(1)}, bf16[2,1024,256]{2,1,0:T(8,128)(2,1)}, u32[]{:S(2)}) copy-start(bf16[2,1024,256]{2,1,0:T(8,128)(2,1)} %all-gather.3.cloned.1.call-done) | copy-start | bytes 3145732
  32.9 2.7 %copy-start.2 = (s32[4]{0:T(128)S(1)}, s32[4]{0:T(128)}, u32[]{:S(2)}) copy-start(s32[4]{0:T(128)} %param.15) | copy-start | bytes 52
  35.6 77.0 %all-reduce.3.cloned.1.call-start = ((), (), s32[]{:S(2)}) async-start(), calls=%async_computation.2 | async-start | bytes 1048576 | tf_op jit(solution)/shard_map/psum | solution.py:40
  83.9 28.7 %copy-start.1 = (bf16[2,256,256]{2,1,0:T(8,128)(2,1)S(1)}, bf16[2,256,256]{2,1,0:T(8,128)(2,1)}, u32[]{:S(2)}) copy-start(bf16[2,256,256]{2,1,0:T(8,128)(2,1)} %param.8) | copy-start | bytes 786436
  83.9 28.7 %copy-start.3 = (f32[2]{0:T(128)S(1)}, f32[2]{0:T(128)}, u32[]{:S(2)}) copy-start(f32[2]{0:T(128)} %param.9) | copy-start | bytes 28
Sparse Core Ops, SparseCore 0:
  10.1 19.4 all-gather.2
  35.7 45.6 all-gather.4
  85.1 27.4 all-reduce.2
where the time goes:
time: 159 us; the launch traced here: 158 us
  waiting for transfers between devices  80.8 us (51%)
  blocking collectives  33.8 us (21%)
  between operations  23 us (14%)
  other arithmetic  11 us (7%)
  matrix products  7.45 us (5%)
  local copies, waits for them, and re-layouts  2.17 us (1%)
    all_gather x1, waiting for transfers between devices, per_device(): lax.all_gather(products, 'cols', axis=2, tiled=True)  42.7 us
    psum x1, blocking collectives, per_device(): lax.psum((jnp.sum(live_f * full_sigma), jnp.sum(live_f * live_f)), ('rows...  33.8 us
    psum x1, waiting for transfers between devices, per_device(): summed = lax.psum(partial_value, 'terms')  27.6 us
    all_gather x1, waiting for transfers between devices, per_device(): panels = lax.all_gather(live_psi, 'rows', axis=1, tiled=True)  10.4 us
    dot_general x4, matrix products, per_device(): jnp.dot(left_ops[term_index], col_panel, preferred_element_type=jnp.float32)  5 us
  transfers between devices with their start and end apart: 3, of which 3 were waited for; matrix products, arithmetic and copies ran while one was open for 3% of the time, Pallas kernels for 0%

commit v1 on v0

--- a/solution.py
+++ b/solution.py
@@ -4,6 +4,12 @@
 from jax.sharding import PartitionSpec as P
 
 EPSILON = 1e-06
+
+
+def add_all(shard, mesh_axis):
+    parts = lax.all_gather(shard, mesh_axis, axis=0, tiled=False)
+    total = parts.sum(axis=0)
+    return total
 
 
 def per_device(wavefunction, energy, block_rows, block_cols, left_ops, right_ops, source, target):
@@ -37,7 +43,7 @@
         hit = (sector_ids == target[term_index])[:, None, None]
         partial_value = partial_value + jnp.where(hit, additions[term_index][None], 0.0)
     live_f = live_psi.astype(jnp.float32)
-    summed = lax.psum(partial_value, "terms")
+    summed = add_all(partial_value, "terms")
     full_sigma = jnp.where(inside, summed + energy[:, None, None] * live_f, 0.0)
     numerator, denominator = lax.psum(
         (jnp.sum(live_f * full_sigma), jnp.sum(live_f * live_f)), ("rows", "cols")

time: 159 us -> 151 us (0.950)
  waiting for transfers between devices: 80.8 us -> 73.4 us
    psum x1 -> x0, waiting for transfers between devices: 27.6 us -> none  [per_device(): summed = lax.psum(partial_value, 'terms')]
    all_gather x0 -> x1, waiting for transfers between devices: none -> 20.2 us  [add_all(): parts = lax.all_gather(shard, mesh_axis, axis=0, tiled=False)]
where the time goes in v1:
time: 151 us; the launch traced here: 150 us
  waiting for transfers between devices  73.4 us (49%)
  blocking collectives  33.8 us (22%)
  between operations  23 us (15%)
  other arithmetic  10.3 us (7%)
  matrix products  7.45 us (5%)
  local copies, waits for them, and re-layouts  2.17 us (1%)
    all_gather x1, waiting for transfers between devices, per_device(): lax.all_gather(products, 'cols', axis=2, tiled=True)  42.7 us
    psum x1, blocking collectives, per_device(): lax.psum((jnp.sum(live_f * full_sigma), jnp.sum(live_f * live_f)), ('rows...  33.8 us
    all_gather x1, waiting for transfers between devices, add_all(): parts = lax.all_gather(shard, mesh_axis, axis=0, tiled=False)  20.2 us
    all_gather x1, waiting for transfers between devices, per_device(): panels = lax.all_gather(live_psi, 'rows', axis=1, tiled=True)  10.4 us
    dot_general x4, matrix products, per_device(): jnp.dot(left_ops[term_index], col_panel, preferred_element_type=jnp.float32)  5 us
  transfers between devices with their start and end apart: 3, of which 3 were waited for; matrix products, arithmetic and copies ran while one was open for 3% of the time, Pallas kernels for 0%

profile of v1, /device:TPU:0, one launch (start us, length us, event | category | flops | bytes accessed | tf_op | source)
XLA Modules:
  0.0 150.2 jit_solution(420277517362419652)
XLA Ops:
  7.2 0.0 copy-start
  7.2 0.0 all-gather.4.cloned.1.call-start
  7.3 0.9 broadcast_compare_fusion
  8.1 1.8 %and_select_fusion.1 = bf16[2,256,256]{2,1,0:T(8,128)(2,1)} fusion(bf16[2,256,256]{2,1,0:T(8,128)(2,1)} %param.8, pred[2,256]{1,0:T(4,128)(4,1)S(1)} %get-tuple-element.20, pred[2,256]{1,0:T(4,128)(4,1)S(1)} %get-tuple-element.21), kind=kLoop, calls=%fused_computation.13 | loop fusion | flops 262144 | bytes 525312 | tf_op jit(solution)/shard_map/jit(_where)/select_n | solution.py:23
  9.9 0.0 all-gather.4.cloned.1.call-update
  10.0 0.0 all-gather.6.cloned.1.call-start
  10.0 1.5 fusion.31
  19.3 10.4 %all-gather.4.cloned.1.call-done = bf16[2,1024,256]{2,1,0:T(8,128)(2,1)} async-done(((bf16[2,256,256]{2,1,0:T(8,128)(2,1)}), bf16[2,1024,256]{2,1,0:T(8,128)(2,1)}) %all-gather.4.cloned.1.call-update) | async-done | bytes 1048592 | tf_op jit(solution)/shard_map/all_gather | solution.py:26
  29.6 0.0 copy-start.4
  29.6 0.0 copy-start.5
  29.6 1.7 %fusion = bf16[1,256,256]{1,2,0:T(8,128)(2,1)S(1)} fusion(bf16[4,256,1024]{2,1,0:T(8,128)(2,1)} %param.12, bf16[2,1024,256]{2,1,0:T(8,128)(2,1)} %all-gather.4.cloned.1.call-done, s32[]{:T(128)S(6)} %select_n.63), kind=kOutput, calls=%fused_computation.4 | convolution fusion | flops 134283264 | bytes 1179652 | tf_op jit(solution)/shard_map/dot_general | solution.py:31
  31.3 1.6 %fusion.1 = bf16[1,256,256]{1,2,0:T(8,128)(2,1)S(1)} fusion(bf16[4,256,1024]{2,1,0:T(8,128)(2,1)} %param.12, bf16[2,1024,256]{2,1,0:T(8,128)(2,1)} %all-gather.4.cloned.1.call-done, s32[]{:T(128)S(6)} %select_n.64), kind=kOutput, calls=%fused_computation.5 | convolution fusion | flops 134283264 | bytes 1179652 | tf_op jit(solution)/shard_map/dot_general | solution.py:31
  32.9 0.0 copy-done.4
  32.9 0.0 copy-start.2
  32.9 1.4 fusion.2
  34.3 0.0 copy-done.5
  34.3 0.4 fusion.3
  34.7 0.9 pad_maximum_fusion
  35.6 0.0 all-gather.6.cloned.1.call-update
  35.6 0.0 all-gather.8.cloned.1.call-start
  35.6 0.0 copy-done.2
  35.7 0.6 fusion.30
  36.2 1.1 iota_compare_fusion
  37.4 1.3 iota_compare_fusion.2
  38.7 42.7 %all-gather.6.cloned.1.call-done = bf16[4,256,1024]{1,2,0:T(8,128)(2,1)} async-done(((bf16[4,256,256]{1,2,0:T(8,128)(2,1)}), bf16[4,256,1024]{1,2,0:T(8,128)(2,1)}) %all-gather.6.cloned.1.call-update) | async-done | bytes 2097168 | tf_op jit(solution)/shard_map/all_gather | solution.py:38
  81.4 0.0 copy-done
  81.4 2.4 %fusion.32 = f32[4,256,256]{2,1,0:T(8,128)S(1)} fusion(bf16[4,256,1024]{1,2,0:T(8,128)(2,1)} %all-gather.6.cloned.1.call-done, bf16[4,256,1024]{2,1,0:T(8,128)(2,1)S(1)} %copy-done), kind=kOutput, calls=%fused_computation.56 | convolution fusion | flops 536870912 | bytes 5242880 | tf_op jit(solution)/shard_map/txl,tml->txm/dot_general | solution.py:36
  83.9 0.1 slice_bitcast_fusion.3
  83.9 0.0 copy-start.1
  84.0 0.0 copy-start.3
  84.0 1.0 select_add_fusion
  85.0 0.0 all-gather.8.cloned.1.call-update
  85.0 20.2 %all-gather.8.cloned.1.call-done = f32[2,2,256,256]{3,2,1,0:T(8,128)} async-done(((f32[1,2,256,256]{3,2,1,0:T(8,128)}), f32[2,2,256,256]{3,2,1,0:T(8,128)}) %all-gather.8.cloned.1.call-update) | async-done | bytes 1048592 | tf_op jit(solution)/shard_map/all_gather | solution.py:10
  105.2 1.4 reduce_sum.27
  106.6 0.0 copy-done.1
  106.6 0.0 copy-done.3
  106.6 0.9 fusion.6
  107.6 33.8 %all-reduce = (f32[]{:T(128)}, f32[]{:T(128)}) all-reduce(f32[]{:T(128)} %get-tuple-element.3, f32[]{:T(128)} %get-tuple-element.2), channel_id=1, replica_groups=mesh['terms'=2,'rows'=4,'cols'=4] {'rows','cols'}, use_global_device_ids=true, to_apply=%region_2.3 | all-reduce | flops 2 | bytes 16 | tf_op jit(solution)/shard_map/psum | solution.py:48
  142.6 1.0 fusion.8
  (2 shorter events, 0.0 us)
Async XLA Ops:
  7.2 74.2 %copy-start = (bf16[4,256,1024]{2,1,0:T(8,128)(2,1)S(1)}, bf16[4,256,1024]{2,1,0:T(8,128)(2,1)}, u32[]{:S(2)}) copy-start(bf16[4,256,1024]{2,1,0:T(8,128)(2,1)} %param.13) | copy-start | bytes 6291460
  7.2 22.4 %all-gather.4.cloned.1.call-start = ((), (), s32[]{:S(2)}) async-start(), calls=%async_computation | async-start | bytes 1310720 | tf_op jit(solution)/shard_map/all_gather | solution.py:26
  10.0 71.4 %all-gather.6.cloned.1.call-start = ((), (), s32[]{:S(2)}) async-start(), calls=%async_computation.1 | async-start | bytes 2621440 | tf_op jit(solution)/shard_map/all_gather | solution.py:38
  29.6 3.3 %copy-start.4 = (bf16[4,256,1024]{2,1,0:T(8,128)(2,1)S(1)}, bf16[4,256,1024]{2,1,0:T(8,128)(2,1)}, u32[]{:S(2)}) copy-start(bf16[4,256,1024]{2,1,0:T(8,128)(2,1)} %param.12) | copy-start | bytes 6291460
  29.6 4.7 %copy-start.5 = (bf16[2,1024,256]{2,1,0:T(8,128)(2,1)S(1)}, bf16[2,1024,256]{2,1,0:T(8,128)(2,1)}, u32[]{:S(2)}) copy-start(bf16[2,1024,256]{2,1,0:T(8,128)(2,1)} %all-gather.4.cloned.1.call-done) | copy-start | bytes 3145732
  32.9 2.7 %copy-start.2 = (s32[4]{0:T(128)S(1)}, s32[4]{0:T(128)}, u32[]{:S(2)}) copy-start(s32[4]{0:T(128)} %param.15) | copy-start | bytes 52
  35.6 69.6 %all-gather.8.cloned.1.call-start = ((), (), s32[]{:S(2)}) async-start(), calls=%async_computation.2 | async-start | bytes 1572864 | tf_op jit(solution)/shard_map/all_gather | solution.py:10
  83.9 22.7 %copy-start.1 = (bf16[2,256,256]{2,1,0:T(8,128)(2,1)S(1)}, bf16[2,256,256]{2,1,0:T(8,128)(2,1)}, u32[]{:S(2)}) copy-start(bf16[2,256,256]{2,1,0:T(8,128)(2,1)} %param.8) | copy-start | bytes 786436
  84.0 22.7 %copy-start.3 = (f32[2]{0:T(128)S(1)}, f32[2]{0:T(128)}, u32[]{:S(2)}) copy-start(f32[2]{0:T(128)} %param.9) | copy-start | bytes 28
Sparse Core Ops, SparseCore 0:
  10.1 19.4 all-gather.3
  35.7 45.6 all-gather.5
  85.1 20.0 all-gather.7
